TPU v7x, 256 devices: a whole 4x4x8 slice. The times are simulated.
256 devices in a mesh: vocab: 256 (over x, y, z, core).
Axes of the slice: x: 4, y: 4, z: 8, core: 2. Of those that a mesh axis runs over, the one named last changes fastest.
Arguments:
- hidden: bfloat16 [2, 256, 3584], P(None, 'vocab'), may hold values from -256 to 256
- head_weight: bfloat16 [3584, 196608], P(None, 'vocab'), may hold values from -1 to 1
- teacher: bfloat16 [2, 256, 196608], P(None, None, 'vocab'), may hold values from 0 to 1
Outputs:
- token_loss: float32 [2, 256], P(None, 'vocab')
- hidden_grad: bfloat16 [2, 256, 3584], P(None, 'vocab')
- head_grad: bfloat16 [3584, 196608], P(None, 'vocab')
All inputs are finite; a program needn't handle non-finite values.
Results may differ from a plain program's by a relative error of at most 0.012.
Values may be sent and summed in bfloat16 or wider, within the bound.
A program may use at most 128 MiB of HBM per device.

v0:
```python
import jax
import jax.numpy as jnp
from jax import lax
from jax.sharding import Mesh
from jax.sharding import PartitionSpec as P

VOCAB = ("vocab_0", "vocab_1", "vocab_2", "vocab_3")


def gathered_once(value, axis):
    leaves = jax.tree.leaves(value)
    order = sorted(range(len(leaves)), key=lambda k: -leaves[k].size)
    width = (1, *leaves[order[0]].shape)[-1]
    lines = [
        jnp.pad(leaves[k].reshape(-1), (0, -leaves[k].size % width)).reshape(-1, width)
        for k in order
    ]
    both, at, found = (lax.all_gather(jnp.concatenate(lines), axis), 0, {})
    for k, line in zip(order, lines):
        slab = both[:, at : at + len(line)].reshape(len(both), -1)
        found[k] = slab[:, : leaves[k].size].reshape(-1, *leaves[k].shape)
        at += len(line)
    numbers = iter(range(len(leaves)))
    return jax.tree.map(lambda _: found[next(numbers)], value)


def joined_all(value, axes, combine):
    for axis in axes:
        pieces = gathered_once(value, axis)
        value = jax.tree.map(lambda part: part[0], pieces)
        for k in range(1, lax.axis_size(axis)):
            value = combine(value, jax.tree.map(lambda part: part[k], pieces))
    return value


def combine_rows(first, second):
    first_peak, first_total, first_mass, first_cross = first
    second_peak, second_total, second_mass, second_cross = second
    joined_peak = jnp.maximum(first_peak, second_peak)
    joined_total = first_total * jnp.exp(first_peak - joined_peak) + second_total * jnp.exp(
        second_peak - joined_peak
    )
    return (joined_peak, joined_total, first_mass + second_mass, first_cross + second_cross)


def finish(logit_block, target_block):
    target_wide = target_block.astype(jnp.float32)
    teacher_mass = jnp.sum(target_wide, axis=-1)
    cross_term = jnp.sum(target_wide * logit_block, axis=-1)
    peak_logit = jnp.max(logit_block, axis=-1)
    exp_total = jnp.sum(jnp.exp(logit_block - peak_logit[..., None]), axis=-1)
    peak_logit, exp_total, teacher_mass, cross_term = joined_all(
        (peak_logit, exp_total, teacher_mass, cross_term), VOCAB, combine_rows
    )
    log_norm = peak_logit + jnp.log(exp_total)
    token_loss = teacher_mass * log_norm - cross_term
    logit_grad = (
        teacher_mass[..., None] * jnp.exp(logit_block - log_norm[..., None]) - target_wide
    ).astype(jnp.bfloat16)
    return (token_loss, logit_grad)


def shards(hidden, head_weight, teacher):
    group_count, row_count, model_width = hidden.shape
    contract = (((1,), (1,)), ((), ()))
    shard_rows = lax.all_gather(hidden, VOCAB, axis=1, tiled=True)
    logits = jnp.einsum("crd,dv->crv", shard_rows, head_weight, preferred_element_type=jnp.float32)
    token_loss, logit_grad = finish(logits, teacher)
    row_total = lax.axis_size(VOCAB) * (group_count * row_count)
    per_group = row_total // group_count
    owner_count = per_group // row_count
    grad_block = logit_grad
    grad_block = (
        grad_block.reshape(group_count, owner_count, row_count, -1)
        .transpose(1, 0, 2, 3)
        .reshape(row_total, -1)
    )
    summed = lax.psum_scatter(
        lax.dot_general(grad_block, head_weight, contract, preferred_element_type=jnp.float32),
        VOCAB,
        scatter_dimension=0,
        tiled=True,
    )
    hidden_grad = summed.reshape(group_count, row_count, model_width).astype(jnp.bfloat16)
    weight_grad = jnp.zeros((model_width, head_weight.shape[1]), jnp.bfloat16)
    for group_index in range(group_count):
        product_term = lax.dot_general(
            shard_rows[group_index],
            logit_grad[group_index],
            (((0,), (0,)), ((), ())),
            preferred_element_type=jnp.float32,
        )
        weight_grad = (weight_grad.astype(jnp.float32) + product_term).astype(jnp.bfloat16)
    own_loss = lax.dynamic_slice_in_dim(token_loss, lax.axis_index(VOCAB) * row_count, row_count, 1)
    return (own_loss, hidden_grad, weight_grad)


def solution(mesh):
    split = Mesh(mesh.devices.reshape(4, 4, 8, 2), ("vocab_0", "vocab_1", "vocab_2", "vocab_3"))
    return jax.shard_map(
        shards,
        mesh=split,
        in_specs=(P(None, VOCAB, None), P(None, VOCAB), P(None, None, VOCAB)),
        out_specs=(P(None, VOCAB), P(None, VOCAB, None), P(None, VOCAB)),
        check_vma=False,
    )
```

profile of v0, /device:TPU:0, one launch (start us, length us, event | category | flops | bytes accessed | tf_op | source)
XLA Modules:
  0.0 362.5 jit_solution(12112623471678827758)
XLA Ops:
  7.2 0.0 all-gather.6.cloned.1.call-start
  7.2 0.7 all-gather.6.cloned.1.call-update
  7.9 0.0 copy-start
  7.9 120.6 %all-gather.6.cloned.1.call-done = bf16[2,256,3584]{2,0,1:T(2,128)(2,1)} async-done(((bf16[2,1,3584]{2,0,1:T(2,128)(2,1)}), bf16[2,256,3584]{2,0,1:T(2,128)(2,1)}) %all-gather.6.cloned.1.call-update) | async-done | bytes 3670032 | tf_op jit(solution)/shard_map/all_gather | solution.py:66
  128.5 6.8 %fusion.76 = (f32[2,256]{1,0:T(2,128)S(1)}, f32[2,256,768]{2,1,0:T(8,128)S(1)}) fusion(bf16[3584,768]{1,0:T(8,128)(2,1)} %param.4, bf16[2,256,3584]{2,0,1:T(2,128)(2,1)} %all-gather.6.cloned.1.call-done), kind=kOutput, calls=%fused_computation.155 | convolution fusion | flops 2818964992 | bytes 10749952 | tf_op jit(solution)/shard_map/crd,dv->crv/dot_general | solution.py:67
  135.2 0.0 copy-done
  135.2 0.7 exponential_reduce_fusion
  136.0 11.9 %all-gather = f32[32,256]{1,0:T(8,128)S(1)} all-gather(f32[8,256]{1,0:T(8,128)S(1)} %pad_maximum_fusion), channel_id=2, replica_groups=mesh['vocab_0'=4,'vocab_1'=4,'vocab_2'=8,'vocab_3'=2] {'vocab_0'}, dimensions={0}, use_global_device_ids=true | all-gather | bytes 40960 | tf_op jit(solution)/shard_map/all_gather | solution.py:18
  148.0 12.3 %all-gather.1 = f32[32,256]{1,0:T(8,128)S(1)} all-gather(f32[8,256]{1,0:T(8,128)S(1)} %pad_maximum_fusion.1), channel_id=3, replica_groups=mesh['vocab_0'=4,'vocab_1'=4,'vocab_2'=8,'vocab_3'=2] {'vocab_1'}, dimensions={0}, use_global_device_ids=true | all-gather | bytes 40960 | tf_op jit(solution)/shard_map/all_gather | solution.py:18
  160.3 24.6 %all-gather.2 = f32[64,256]{1,0:T(8,128)S(1)} all-gather(f32[8,256]{1,0:T(8,128)S(1)} %pad_maximum_fusion.2), channel_id=4, replica_groups=mesh['vocab_0'=4,'vocab_1'=4,'vocab_2'=8,'vocab_3'=2] {'vocab_2'}, dimensions={0}, use_global_device_ids=true | all-gather | bytes 73728 | tf_op jit(solution)/shard_map/all_gather | solution.py:18
  185.0 1.8 all-gather.3
  186.8 0.4 fusion.4
  187.2 0.1 dynamic-slice_subtract_fusion
  187.3 0.6 copy.22
  187.9 0.8 copy.19
  188.7 0.3 reshape.111
  189.0 7.7 %fusion.77 = f32[512,3584]{1,0:T(8,128)} fusion(bf16[512,768]{1,0:T(8,128)(2,1)S(1)} %reshape.111, bf16[3584,768]{1,0:T(8,128)(2,1)} %param.4), kind=kOutput, calls=%fused_computation.156 | convolution fusion | flops 2818572288 | bytes 13631488 | tf_op jit(solution)/shard_map/dot_general | solution.py:79
  196.7 141.2 %all-reduce.2 = bf16[512,3584]{1,0:T(8,128)(2,1)} all-reduce(f32[512,3584]{1,0:T(8,128)} %fusion.77), channel_id=6, replica_groups=mesh['vocab_0'=4,'vocab_1'=4,'vocab_2'=8,'vocab_3'=2] {'vocab_0','vocab_..., use_global_device_ids=true, to_apply=%region_4.5.clone | all-reduce | flops 1835008 | bytes 11010048
  337.9 2.4 copy.18
  340.3 1.6 convolution_convert_fusion
  341.9 4.1 %fusion = bf16[3584,768]{0,1:T(8,128)(2,1)} fusion(bf16[768,3584]{1,0:T(8,128)(2,1)S(1)} %convolution_convert_fusion, bf16[2,256,3584]{2,1,0:T(8,128)(2,1)S(1)} %copy.18, bf16[2,256,768]{2,1,0:T(8,128)(2,1)S(1)} %fusion.4), kind=kOutput, calls=%fused_computation.2 | convolution fusion | flops 1417543680 | bytes 13238272 | tf_op jit(solution)/shard_map/dot_general | solution.py:87
  345.9 8.3 %copy.23 = bf16[3584,768]{1,0:T(8,128)(2,1)} copy(bf16[3584,768]{0,1:T(8,128)(2,1)} %fusion) | data formatting | bytes 11010048
  354.2 1.4 fusion.5
  (12 shorter events, 0.2 us)
Async XLA Ops:
  7.2 121.3 %all-gather.6.cloned.1.call-start = ((), (), s32[]{:S(2)}) async-start(), calls=%async_computation | async-start | bytes 3684352 | tf_op jit(solution)/shard_map/all_gather | solution.py:66
  7.9 127.3 %copy-start = (bf16[2,256,768]{2,1,0:T(8,128)(2,1)S(1)}, bf16[2,256,768]{2,1,0:T(8,128)(2,1)}, u32[]{:S(2)}) copy-start(bf16[2,256,768]{2,1,0:T(8,128)(2,1)} %param.5) | copy-start | bytes 2359300
Sparse Core Ops, SparseCore 0:
  11.8 116.5 all-gather.5
where the time goes:
time: 363 us; the launch traced here: 362 us
  blocking collectives  192 us (53%)
  waiting for transfers between devices  121 us (33%)
  matrix products  20.1 us (6%)
  between operations  14.2 us (4%)
  local copies, waits for them, and re-layouts  13.8 us (4%)
    unnamed x1, blocking collectives  141 us
    all_gather x1, waiting for transfers between devices, shards(): shard_rows = lax.all_gather(hidden, VOCAB, axis=1, tiled=True)  121 us
    all_gather x4, blocking collectives, gathered_once(): both, at, found = (lax.all_gather(jnp.concatenate(lines), axis), 0, {})  50.6 us
    unnamed x4, local copies, waits for them, and re-layouts  8.87 us
    dot_general x1, matrix products, shards(): lax.dot_general(grad_block, head_weight, contract, preferred_element_type...  7.67 us
  transfers between devices with their start and end apart: 1, of which 1 were waited for; matrix products, arithmetic and copies ran while one was open for 0% of the time, Pallas kernels for 0%

commit v1 on v0

--- a/solution.py
+++ b/solution.py
@@ -63,7 +63,9 @@
 def shards(hidden, head_weight, teacher):
     group_count, row_count, model_width = hidden.shape
     contract = (((1,), (1,)), ((), ()))
-    shard_rows = lax.all_gather(hidden, VOCAB, axis=1, tiled=True)
+    shard_rows = jnp.concatenate(
+        lax.all_to_all(jnp.stack([hidden] * lax.axis_size(VOCAB)), VOCAB, 0, 0), axis=1
+    )
     logits = jnp.einsum("crd,dv->crv", shard_rows, head_weight, preferred_element_type=jnp.float32)
     token_loss, logit_grad = finish(logits, teacher)
     row_total = lax.axis_size(VOCAB) * (group_count * row_count)

time: 363 us -> 331 us (0.912)
  waiting for transfers between devices: 121 us -> 82 us
  starting transfers between devices: 0.04 us -> 15.5 us
  between operations: 14.2 us -> 0.77 us
  local copies, waits for them, and re-layouts: 13.8 us -> 18.2 us
    all_gather x1 -> x0, waiting for transfers between devices: 121 us -> none  [shards(): shard_rows = lax.all_gather(hidden, VOCAB, axis=1, tiled=True)]
    all_to_all x0 -> x1, waiting for transfers between devices: none -> 82 us  [shards(): lax.all_to_all(jnp.stack([hidden] * lax.axis_size(VOCAB)), VOCAB, 0, 0)]
    all_to_all x0 -> x1, starting transfers between devices: none -> 15.5 us  [shards(): lax.all_to_all(jnp.stack([hidden] * lax.axis_size(VOCAB)), VOCAB, 0, 0)]
    another operation x0 -> x1, local copies, waits for them, and re-layouts: none -> 4.44 us  [shards(): jnp.stack([hidden] * lax.axis_size(VOCAB))]
where the time goes in v1:
time: 331 us; the launch traced here: 330 us
  blocking collectives  192 us (58%)
  waiting for transfers between devices  82 us (25%)
  matrix products  20.1 us (6%)
  local copies, waits for them, and re-layouts  18.2 us (5%)
  starting transfers between devices  15.5 us (5%)
    unnamed x1, blocking collectives  140 us
    all_to_all x1, waiting for transfers between devices, shards(): lax.all_to_all(jnp.stack([hidden] * lax.axis_size(VOCAB)), VOCAB, 0, 0)  82 us
    all_gather x4, blocking collectives, gathered_once(): both, at, found = (lax.all_gather(jnp.concatenate(lines), axis), 0, {})  52.2 us
    all_to_all x1, starting transfers between devices, shards(): lax.all_to_all(jnp.stack([hidden] * lax.axis_size(VOCAB)), VOCAB, 0, 0)  15.5 us
    unnamed x4, local copies, waits for them, and re-layouts  8.87 us
    dot_general x1, matrix products, shards(): lax.dot_general(grad_block, head_weight, contract, preferred_element_type...  7.67 us
    dot_general x1, matrix products, shards(): jnp.einsum('crd,dv->crv', shard_rows, head_weight, preferred_element_type...  6.76 us
  transfers between devices with their start and end apart: 1, of which 1 were waited for; matrix products, arithmetic and copies ran while one was open for 0% of the time, Pallas kernels for 0%

profile of v1, /device:TPU:0, one launch (start us, length us, event | category | flops | bytes accessed | tf_op | source)
XLA Modules:
  0.0 329.9 jit_solution(13470131108202146585)
XLA Ops:
  0.6 4.4 %stack.2 = bf16[256,2,1,3584]{3,1,2,0:T(2,128)(2,1)} broadcast(bf16[2,3584]{1,0:T(2,128)(2,1)} %bitcast.393), dimensions={1,3} | broadcast | bytes 3684352 | tf_op jit(solution)/shard_map/stack | solution.py:67
  5.1 15.5 %all-to-all-start = ((bf16[256,2,1,3584]{3,1,2,0:T(2,128)(2,1)}), bf16[256,2,1,3584]{3,1,2,0:T(2,128)(2,1)}, u32[]{:S(2)}, u32[]{:S(2)}) async-start(bf16[256,2,1,3584]{3,1,2,0:T(2,128)(2,1)} %stack.2), calls=%async_computation | async-start | bytes 7340032 | tf_op jit(solution)/shard_map/all_to_all | solution.py:67
  20.6 0.0 copy-start
  20.6 82.0 %all-to-all-done = bf16[256,2,1,3584]{3,1,2,0:T(2,128)(2,1)} async-done(((bf16[256,2,1,3584]{3,1,2,0:T(2,128)(2,1)}), bf16[256,2,1,3584]{3,1,2,0:T(2,128)(2,1)}, u32[]{:S(2)}, u32[]{:S(2)}) %all-to-all-start) | async-done | bytes 3670048 | tf_op jit(solution)/shard_map/all_to_all | solution.py:67
  102.6 6.8 %fusion.77 = (f32[2,256]{1,0:T(2,128)S(1)}, f32[2,256,768]{2,1,0:T(8,128)S(1)}) fusion(bf16[3584,768]{1,0:T(8,128)(2,1)} %param.4, bf16[256,2,1,3584]{3,1,2,0:T(2,128)(2,1)} %all-to-all-done), kind=kOutput, calls=%fused_computation.157 | convolution fusion | flops 2818964992 | bytes 10749952 | tf_op jit(solution)/shard_map/crd,dv->crv/dot_general | solution.py:69
  109.4 0.0 copy-done
  109.4 0.7 exponential_reduce_fusion
  110.1 11.9 %all-gather = f32[32,256]{1,0:T(8,128)S(1)} all-gather(f32[8,256]{1,0:T(8,128)S(1)} %pad_maximum_fusion), channel_id=2, replica_groups=mesh['vocab_0'=4,'vocab_1'=4,'vocab_2'=8,'vocab_3'=2] {'vocab_0'}, dimensions={0}, use_global_device_ids=true | all-gather | bytes 40960 | tf_op jit(solution)/shard_map/all_gather | solution.py:18
  122.1 12.5 %all-gather.1 = f32[32,256]{1,0:T(8,128)S(1)} all-gather(f32[8,256]{1,0:T(8,128)S(1)} %pad_maximum_fusion.1), channel_id=3, replica_groups=mesh['vocab_0'=4,'vocab_1'=4,'vocab_2'=8,'vocab_3'=2] {'vocab_1'}, dimensions={0}, use_global_device_ids=true | all-gather | bytes 40960 | tf_op jit(solution)/shard_map/all_gather | solution.py:18
  134.7 26.0 %all-gather.2 = f32[64,256]{1,0:T(8,128)S(1)} all-gather(f32[8,256]{1,0:T(8,128)S(1)} %pad_maximum_fusion.2), channel_id=4, replica_groups=mesh['vocab_0'=4,'vocab_1'=4,'vocab_2'=8,'vocab_3'=2] {'vocab_2'}, dimensions={0}, use_global_device_ids=true | all-gather | bytes 73728 | tf_op jit(solution)/shard_map/all_gather | solution.py:18
  160.7 1.8 all-gather.3
  162.5 0.4 fusion.6
  163.0 0.1 dynamic-slice_subtract_fusion
  163.0 0.6 copy.14
  163.6 0.8 copy.13
  164.5 0.3 reshape.126
  164.8 7.7 %fusion.78 = f32[512,3584]{1,0:T(8,128)} fusion(bf16[512,768]{1,0:T(8,128)(2,1)S(1)} %reshape.126, bf16[3584,768]{1,0:T(8,128)(2,1)} %param.4), kind=kOutput, calls=%fused_computation.158 | convolution fusion | flops 2818572288 | bytes 13631488 | tf_op jit(solution)/shard_map/dot_general | solution.py:81
  172.4 139.7 %all-reduce.2 = bf16[512,3584]{1,0:T(8,128)(2,1)} all-reduce(f32[512,3584]{1,0:T(8,128)} %fusion.78), channel_id=6, replica_groups=mesh['vocab_0'=4,'vocab_1'=4,'vocab_2'=8,'vocab_3'=2] {'vocab_0','vocab_..., use_global_device_ids=true, to_apply=%region_4.5.clone | all-reduce | flops 1835008 | bytes 11010048
  312.1 2.4 copy.23
  314.5 1.6 convolution_convert_fusion
  316.2 4.1 %fusion = bf16[3584,768]{0,1:T(8,128)(2,1)} fusion(bf16[768,3584]{1,0:T(8,128)(2,1)S(1)} %convolution_convert_fusion, bf16[2,256,1,3584]{3,1,0,2:T(8,128)(2,1)S(1)} %bitcast.383, bf16[2,256,768]{2,1,0:T(8,128)(2,1)S(1)} %fusion.6), kind=kOutput, calls=%fused_computation.2 | convolution fusion | flops 1417543680 | bytes 13238272 | tf_op jit(solution)/shard_map/dot_general | solution.py:89
  320.2 8.3 %copy.15 = bf16[3584,768]{1,0:T(8,128)(2,1)} copy(bf16[3584,768]{0,1:T(8,128)(2,1)} %fusion) | data formatting | bytes 11010048
  328.5 1.4 fusion.7
  (12 shorter events, 0.2 us)
Async XLA Ops:
  5.1 97.6 %all-to-all-start = ((bf16[256,2,1,3584]{3,1,2,0:T(2,128)(2,1)}), bf16[256,2,1,3584]{3,1,2,0:T(2,128)(2,1)}, u32[]{:S(2)}, u32[]{:S(2)}) async-start(bf16[256,2,1,3584]{3,1,2,0:T(2,128)(2,1)} %stack.2), calls=%async_computation | async-start | bytes 7340032 | tf_op jit(solution)/shard_map/all_to_all | solution.py:67
  20.6 88.8 %copy-start = (bf16[2,256,768]{2,1,0:T(8,128)(2,1)S(1)}, bf16[2,256,768]{2,1,0:T(8,128)(2,1)}, u32[]{:S(2)}) copy-start(bf16[2,256,768]{2,1,0:T(8,128)(2,1)} %param.5) | copy-start | bytes 2359300
